TPU v7x, 32 devices: a whole 2x2x4 slice. The times are simulated.
32 devices in a mesh: row: 8 (over y, x, core), col: 4 (over z).
Axes of the slice: x: 2, y: 2, z: 4, core: 2. Of those that a mesh axis runs over, the one named last changes fastest.
Arguments:
- alignment_state: bfloat16 [128, 128, 256], P('col', 'row'), may hold values from -6 to 6
- layer_norm_gain: float32 [256], replicated, may hold values from 0.1 to 1.9
- left_weight_matrix: bfloat16 [256, 32], replicated, may hold values from -0.375 to 0.375
- right_weight_matrix: bfloat16 [256, 32], replicated, may hold values from -0.375 to 0.375
- output_weight_matrix: bfloat16 [1024, 128], replicated, may hold values from -0.1875 to 0.1875
- output_bias_vector: float32 [128], replicated, may hold values from -3 to 3
- pair_update_cotangent: bfloat16 [128, 128, 128], P('row', 'col'), may hold values from -40 to 40
Outputs:
- pair_update_output: bfloat16 [128, 128, 128], P('row', 'col')
- alignment_gradient: bfloat16 [128, 128, 256], P('col', 'row')
- left_weight_gradient: float32 [256, 32], replicated
- right_weight_gradient: float32 [256, 32], replicated
- out_w_grad: float32 [1024, 128], P(('row', 'col'))
- norm_gain_gradient: float32 [256], replicated
- output_bias_gradient: float32 [128], replicated
All inputs are finite; a program needn't handle non-finite values.
Results may differ from a plain program's by a relative error of at most 0.024.
Values may be sent and summed in bfloat16 or wider, within the bound.
No kernel may reach another device: no remote copies, remote signals or barrier semaphores. Data moves between devices by JAX's collectives and lax.ppermute only.
A program may use at most 64 MiB of HBM per device.

v0:
```python
import jax
import jax.numpy as jnp
from jax import lax
from jax.sharding import PartitionSpec as P


def from_root(block, axis, holder):
    block = jnp.where(lax.axis_index(axis) == holder, block, jnp.zeros_like(block))
    return lax.psum(block, axis)


def apply_layer_norm(alignment_state):
    value_entries = alignment_state.astype(jnp.float32)
    center = value_entries - jnp.mean(value_entries, axis=-1, keepdims=True)
    inverse_deviation = lax.rsqrt(jnp.mean(center * center, axis=-1, keepdims=True) + 1e-05)
    return (center * inverse_deviation, inverse_deviation)


def on_device(
    alignment_state,
    layer_norm_gain,
    left_weight_matrix,
    right_weight_matrix,
    output_weight_matrix,
    output_bias_vector,
    pair_update_cotangent,
):
    sequence_block_local, residue_block_local, alignment_weight = alignment_state.shape
    proj_w = left_weight_matrix.shape[1]
    pair_w = output_weight_matrix.shape[1]
    row_count = lax.axis_size("row")
    col_count = lax.axis_size("col")
    row_ratio = row_count // col_count
    total_res = residue_block_local * row_count
    col_res = residue_block_local * row_ratio
    col_index = lax.axis_index("col")
    row_index = lax.axis_index("row")
    normed_alignment, inverse_deviation = apply_layer_norm(alignment_state)
    layer_norm_output = (normed_alignment * layer_norm_gain).astype(jnp.bfloat16)
    normed_flat_rows = layer_norm_output.reshape(-1, alignment_weight)
    left_local = (
        jnp.dot(normed_flat_rows, left_weight_matrix, preferred_element_type=jnp.float32)
        .astype(jnp.bfloat16)
        .reshape(sequence_block_local, residue_block_local, proj_w)
    )
    right_local = (
        jnp.dot(normed_flat_rows, right_weight_matrix, preferred_element_type=jnp.float32)
        .astype(jnp.bfloat16)
        .reshape(sequence_block_local, residue_block_local, proj_w)
    )
    left_all, right_rows = (
        lax.all_gather(left_local, "col", axis=0, tiled=True),
        lax.all_gather(right_local, "col", axis=0, tiled=True),
    )
    seq_total = left_all.shape[0]
    right_every = lax.all_gather(right_rows, "row", axis=1, tiled=True)
    right_block = lax.dynamic_slice_in_dim(right_every, col_index * col_res, col_res, 1)
    block_res = min(8, residue_block_local)

    def visit(totals, row_start):
        right_acc, projection_running_sum = totals
        left_part = lax.dynamic_slice_in_dim(left_all, row_start, block_res, 1)
        cot_part = lax.dynamic_slice_in_dim(pair_update_cotangent, row_start, block_res, 0)
        outer_prod = jnp.einsum(
            "sic,sjd->ijcd", left_part, right_block, preferred_element_type=jnp.float32
        )
        outer_flat = (
            (outer_prod / seq_total)
            .astype(jnp.bfloat16)
            .reshape(block_res * col_res, proj_w * proj_w)
        )
        cot_flat = cot_part.reshape(block_res * col_res, pair_w)
        pair_part = (
            jnp.dot(outer_flat, output_weight_matrix, preferred_element_type=jnp.float32)
            + output_bias_vector
        ).astype(jnp.bfloat16)
        projection_running_sum = projection_running_sum + lax.dot_general(
            outer_flat, cot_flat, (((0,), (0,)), ((), ())), preferred_element_type=jnp.float32
        )
        outer_grad = lax.dot_general(
            cot_flat,
            output_weight_matrix,
            (((1,), (1,)), ((), ())),
            preferred_element_type=jnp.float32,
        ).astype(jnp.bfloat16)
        outer_grad = outer_grad.reshape(block_res, col_res, proj_w, proj_w)
        left_part_grad = (
            jnp.einsum("ijcd,sjd->sic", outer_grad, right_block, preferred_element_type=jnp.float32)
            / seq_total
        )
        right_acc = (
            right_acc
            + jnp.einsum("ijcd,sic->sjd", outer_grad, left_part, preferred_element_type=jnp.float32)
            / seq_total
        )
        return (
            (right_acc, projection_running_sum),
            (pair_part.reshape(block_res, col_res, pair_w), left_part_grad),
        )

    starts = jnp.arange(residue_block_local // block_res, dtype=jnp.int32) * block_res
    initial = (
        jnp.zeros((seq_total, col_res, proj_w), jnp.float32),
        jnp.zeros((proj_w * proj_w, pair_w), jnp.float32),
    )
    (right_acc, projection_running_sum), (pair_parts, left_parts) = lax.scan(visit, initial, starts)
    pair_update_output = pair_parts.reshape(residue_block_local, col_res, pair_w)
    left_partial = jnp.transpose(left_parts, (1, 0, 2, 3)).reshape(
        seq_total, residue_block_local, proj_w
    )
    left_d = lax.psum_scatter(
        left_partial.astype(jnp.bfloat16), "col", scatter_dimension=0, tiled=True
    )
    right_full = lax.psum(right_acc.astype(jnp.bfloat16), "row").astype(jnp.float32)
    right_half = lax.dynamic_slice_in_dim(
        right_full, row_index % row_ratio * residue_block_local, residue_block_local, 1
    )
    right_home = from_root(right_half.astype(jnp.bfloat16), "col", row_index // row_ratio).astype(
        right_half.dtype
    )
    right_d = lax.dynamic_slice_in_dim(
        right_home, col_index * sequence_block_local, sequence_block_local, 0
    ).astype(jnp.bfloat16)
    left_flat = left_d.reshape(-1, proj_w)
    right_flat = right_d.reshape(-1, proj_w)
    normed_derivative = lax.dot_general(
        left_flat, left_weight_matrix, (((1,), (1,)), ((), ())), preferred_element_type=jnp.float32
    )
    normed_derivative = normed_derivative + lax.dot_general(
        right_flat,
        right_weight_matrix,
        (((1,), (1,)), ((), ())),
        preferred_element_type=jnp.float32,
    )
    normed_derivative = normed_derivative.reshape(
        sequence_block_local, residue_block_local, alignment_weight
    )
    scaled_product = normed_derivative * layer_norm_gain
    alignment_gradient = (
        (
            scaled_product
            - jnp.mean(scaled_product, axis=-1, keepdims=True)
            - normed_alignment * jnp.mean(scaled_product * normed_alignment, axis=-1, keepdims=True)
        )
        * inverse_deviation
    ).astype(jnp.bfloat16)
    weight_left = lax.dot_general(
        normed_flat_rows, left_flat, (((0,), (0,)), ((), ())), preferred_element_type=jnp.float32
    )
    weight_right = lax.dot_general(
        normed_flat_rows, right_flat, (((0,), (0,)), ((), ())), preferred_element_type=jnp.float32
    )
    gain_part = jnp.sum(normed_derivative * normed_alignment, axis=(0, 1))
    bias_part = jnp.sum(pair_update_cotangent, axis=(0, 1), dtype=jnp.float32)
    param_totals = lax.psum((weight_left, weight_right, gain_part, bias_part), ("row", "col"))
    proj_partial = lax.psum_scatter(
        projection_running_sum.astype(jnp.bfloat16), "row", scatter_dimension=0, tiled=True
    ).astype(jnp.float32)
    proj_total = lax.psum_scatter(proj_partial, "col", scatter_dimension=0, tiled=True)
    return (
        pair_update_output,
        alignment_gradient,
        param_totals[0] / total_res,
        param_totals[1] / total_res,
        proj_total / total_res,
        param_totals[2] / total_res,
        param_totals[3] / total_res,
    )


def solution(mesh):
    return jax.shard_map(
        on_device,
        mesh=mesh,
        in_specs=(P("col", "row", None), P(), P(), P(), P(), P(), P("row", "col", None)),
        out_specs=(
            P("row", "col", None),
            P("col", "row", None),
            P(),
            P(),
            P(("row", "col"), None),
            P(),
            P(),
        ),
        check_vma=False,
    )
```

profile of v0, /device:TPU:0, one launch (start us, length us, event | category | flops | bytes accessed | tf_op | source)
XLA Modules:
  0.0 416.1 jit_solution(7871246451103388164)
XLA Ops:
  11.1 18.0 %all_gather.10 = bf16[128,16,32]{2,1,0:T(8,128)(2,1)} all-gather(bf16[32,16,32]{2,1,0:T(8,128)(2,1)S(1)} %bitcast.126), channel_id=1, replica_groups=mesh['row'=8,'col'=4] {'col'}, dimensions={0}, use_global_device_ids=true | all-gather | bytes 163840 | tf_op jit(solution)/shard_map/all_gather | solution.py:53
  29.6 16.3 %all_gather.9 = bf16[128,16,32]{2,1,0:T(8,128)(2,1)S(1)} all-gather(bf16[32,16,32]{2,1,0:T(8,128)(2,1)S(1)} %bitcast.127), channel_id=1, replica_groups=mesh['row'=8,'col'=4] {'col'}, dimensions={0}, use_global_device_ids=true | all-gather | bytes 163840 | tf_op jit(solution)/shard_map/all_gather | solution.py:52
  46.8 21.7 %all-gather.2.cloned.1.call-done = bf16[128,128,32]{2,1,0:T(8,128)(2,1)} async-done(((bf16[128,16,32]{2,1,0:T(8,128)(2,1)}), bf16[128,128,32]{2,1,0:T(8,128)(2,1)}) %all-gather.2.cloned.1.call-update) | async-done | bytes 1048592 | tf_op jit(solution)/shard_map/all_gather | solution.py:56
  68.5 1.3 constant_dynamic-slice_fusion.1
  69.8 1.8 copy.44
  71.6 32.6 %while.17 = (s32[]{:T(128)}, f32[128,32,32]{0,2,1:T(8,128)}, f32[1024,128]{1,0:T(8,128)S(1)}, bf16[2,8,32,128]{3,2,1,0:T(8,128)(2,1)}, bf16[2,128,8,32]{1,3,2,0:...) while((s32[]{:T(128)}, f32[128,32,32]{0,2,1:T(8,128)}, ...), condition=%wide.region_3.4_spmd.clone, body=%wide.region_2.3_spmd.clone.sunk | while | flops 404193280 | bytes 15928666 | solution.py:106
  71.6 1.2 dynamic_slice.46
  74.8 1.7 fusion.79
  76.5 2.2 reshape.95
  81.1 1.6 reshape.94
  82.7 1.5 fusion.78
  85.3 2.1 fusion.81
  87.4 1.2 dynamic_slice.46
  90.6 1.7 fusion.79
  92.2 2.2 reshape.95
  96.9 1.6 reshape.94
  98.5 2.6 fusion.78
  102.1 2.1 fusion.81
  104.3 1.8 convert_element_type.67
  106.2 2.1 copy.45
  109.0 51.2 %all-reduce.5.cloned.1.call-done = bf16[128,32,32]{0,2,1:T(8,128)(2,1)} async-done(((bf16[128,32,32]{0,2,1:T(8,128)(2,1)}), bf16[128,32,32]{0,2,1:T(8,128)(2,1)}) %all-reduce.5.cloned.1.call-update) | async-done | bytes 262160 | tf_op jit(solution)/shard_map/psum | solution.py:114
  160.2 1.6 fusion.28
  161.8 21.9 %reduce-scatter.4.cloned.1.call-done = bf16[32,16,32]{2,1,0:T(8,128)(2,1)} async-done(((bf16[128,16,32]{2,1,0:T(8,128)(2,1)}), bf16[32,16,32]{2,1,0:T(8,128)(2,1)}) %reduce-scatter.4.cloned.1.call-update) | async-done | bytes 32784 | tf_op jit(solution)/shard_map/reduce_scatter | solution.py:111
  184.8 1.7 convolution_bitcast_fusion.3
  186.5 32.9 %all-reduce.7.cloned.1.call-done = bf16[128,16,32]{0,2,1:T(8,128)(2,1)} async-done(((bf16[128,16,32]{0,2,1:T(8,128)(2,1)}), bf16[128,16,32]{0,2,1:T(8,128)(2,1)}) %all-reduce.7.cloned.1.call-update) | async-done | bytes 131088 | tf_op jit(solution)/shard_map/psum | solution.py:9
  224.5 122.1 %all-reduce.9.cloned.1.call-done = (f32[256,32]{0,1:T(8,128)}, f32[256,32]{0,1:T(8,128)}, f32[256]{0:T(256)}, f32[128]{0:T(128)}) async-done(((f32[256,32]{0,1:T(8,128)}, f32[256,32]{0,1:T(8,128)}, f32[256]{0:T(256)}, f32[128]{0:T(128)}), (f32[256,32]{0,1:T(8,128)}, f32[256,32]{0,1:T(8,128)}, f32[256]{0:T(256)}, f32[128]{0:T(128)})) %all-reduce.9.cloned.1.call-update) | async-done | bytes 67088 | tf_op jit(solution)/shard_map/psum | solution.py:155
  346.7 1.2 broadcast_multiply_fusion.6
  347.9 1.4 broadcast_multiply_fusion
  349.3 37.1 %reduce-scatter.6.cloned.1.call-done = bf16[128,128]{1,0:T(8,128)(2,1)} async-done(((bf16[1024,128]{1,0:T(8,128)(2,1)}), bf16[128,128]{1,0:T(8,128)(2,1)}) %reduce-scatter.6.cloned.1.call-update) | async-done | bytes 32784 | tf_op jit(solution)/shard_map/reduce_scatter | solution.py:156
  386.4 1.4 convert_element_type.74
  388.9 19.1 %reduce-scatter.8.cloned.1.call-done = f32[32,128]{1,0:T(8,128)} async-done(((f32[128,128]{1,0:T(8,128)}), f32[32,128]{1,0:T(8,128)}) %reduce-scatter.8.cloned.1.call-update) | async-done | bytes 16400 | tf_op jit(solution)/shard_map/reduce_scatter | solution.py:159
  408.0 1.3 broadcast_multiply_fusion.2
  (98 shorter events, 19.9 us)
Async XLA Ops:
  7.2 3.6 copy-start
  7.2 22.1 %copy-start.12 = (bf16[256,32]{0,1:T(8,128)(2,1)S(1)}, bf16[256,32]{0,1:T(8,128)(2,1)}, u32[]{:S(2)}) copy-start(bf16[256,32]{0,1:T(8,128)(2,1)} %param.11) | copy-start | bytes 49156
  7.2 61.3 %all-gather.2.cloned.1.call-start = ((), (), s32[]{:S(2)}) async-start(), calls=%async_computation.3 | async-start | bytes 4718592 | tf_op jit(solution)/shard_map/all_gather | solution.py:56
  8.3 2.4 copy-start.8
  9.6 1.2 copy-start.10
  10.8 18.8 %copy-start.5 = (bf16[32,16,256]{2,1,0:T(8,128)(2,1)}, bf16[32,16,256]{2,1,0:T(8,128)(2,1)S(1)}, u32[]{:S(2)}) copy-start(bf16[32,16,256]{2,1,0:T(8,128)(2,1)S(1)} %fusion.21) | copy-start | bytes 786436
  29.1 131.0 %all-reduce.5.cloned.1.call-start = ((), (), s32[]{:S(2)}) async-start(), calls=%async_computation.5 | async-start | bytes 524288 | tf_op jit(solution)/shard_map/psum | solution.py:114
  45.9 25.7 %copy-start.1 = (bf16[1024,128]{1,0:T(8,128)(2,1)S(1)}, bf16[1024,128]{1,0:T(8,128)(2,1)}, u32[]{:S(2)}) copy-start(bf16[1024,128]{1,0:T(8,128)(2,1)} %param.13) | copy-start | bytes 786436
  80.0 0.8 copy-start.2
  82.7 1.6 copy-start.15
  82.7 1.9 copy-start.16
  84.3 3.1 copy-start.3
  84.6 0.7 copy-start.17
  95.8 0.8 copy-start.2
  98.5 2.7 copy-start.15
  98.5 2.9 copy-start.16
  101.1 3.1 copy-start.3
  101.5 0.7 copy-start.17
  104.2 4.1 copy-start.7
  104.2 79.5 %copy-start.13 = (bf16[256,32]{0,1:T(8,128)(2,1)S(1)}, bf16[256,32]{0,1:T(8,128)(2,1)}, u32[]{:S(2)}) copy-start(bf16[256,32]{0,1:T(8,128)(2,1)} %param.11) | copy-start | bytes 49156
  104.2 80.6 %copy-start.6 = (bf16[32,16,256]{2,1,0:T(8,128)(2,1)S(1)}, bf16[32,16,256]{2,1,0:T(8,128)(2,1)}, u32[]{:S(2)}) copy-start(bf16[32,16,256]{2,1,0:T(8,128)(2,1)} %copy-done.5) | copy-start | bytes 786436
  106.1 115.3 %copy-start.14 = (f32[256]{0:T(256)S(1)}, f32[256]{0:T(256)}, u32[]{:S(2)}) copy-start(f32[256]{0:T(256)} %param.10) | copy-start | bytes 3076
  106.1 77.6 %reduce-scatter.4.cloned.1.call-start = ((), (), s32[]{:S(2)}) async-start(), calls=%async_computation.4 | async-start | bytes 655360 | tf_op jit(solution)/shard_map/reduce_scatter | solution.py:111
  108.3 113.5 %copy-start.4 = (bf16[32,16,256]{2,1,0:T(8,128)(2,1)S(1)}, bf16[32,16,256]{2,1,0:T(8,128)(2,1)}, u32[]{:S(2)}) copy-start(bf16[32,16,256]{2,1,0:T(8,128)(2,1)} %param.9) | copy-start | bytes 786436
  108.3 113.5 %copy-start.9 = (f32[32,16]{1,0:T(8,128)S(1)}, f32[32,16]{1,0:T(8,128)}, u32[]{:S(2)}) copy-start(f32[32,16]{1,0:T(8,128)} %copy-done.8) | copy-start | bytes 6148
  108.3 113.5 %copy-start.11 = (f32[32,16]{1,0:T(8,128)S(1)}, f32[32,16]{1,0:T(8,128)}, u32[]{:S(2)}) copy-start(f32[32,16]{1,0:T(8,128)} %copy-done.10) | copy-start | bytes 6148
  108.3 111.1 %all-reduce.7.cloned.1.call-start = ((), (), s32[]{:S(2)}) async-start(), calls=%async_computation.6 | async-start | bytes 262144 | tf_op jit(solution)/shard_map/psum | solution.py:9
  161.8 184.9 %all-reduce.9.cloned.1.call-start = ((), (), s32[]{:S(2)}) async-start(), calls=%async_computation.9 | async-start | bytes 134144 | tf_op jit(solution)/shard_map/psum | solution.py:155
  222.5 163.9 %reduce-scatter.6.cloned.1.call-start = ((), (), s32[]{:S(2)}) async-start(), calls=%async_computation.7 | async-start | bytes 294912 | tf_op jit(solution)/shard_map/reduce_scatter | solution.py:156
  223.3 184.6 %reduce-scatter.8.cloned.1.call-start = ((), (), s32[]{:S(2)}) async-start(), calls=%async_computation.8 | async-start | bytes 81920 | tf_op jit(solution)/shard_map/reduce_scatter | solution.py:159
Sparse Core Ops, SparseCore 0:
  29.3 39.2 all-gather.1
  106.2 53.8 all-reduce.4
  162.4 21.2 reduce-scatter.3
  186.5 32.8 all-reduce.6
  225.9 120.6 all-reduce.8
  349.5 36.8 reduce-scatter.5
  388.6 19.2 reduce-scatter.7
where the time goes:
time: 417 us; the launch traced here: 416 us
  waiting for transfers between devices  306 us (73%)
  blocking collectives  34.3 us (8%)
  local copies, waits for them, and re-layouts  21 us (5%)
  matrix products  18.1 us (4%)
  other arithmetic  18 us (4%)
  between operations  14.4 us (3%)
    psum x1, waiting for transfers between devices, on_device(): lax.psum((weight_left, weight_right, gain_part, bias_part), ('row', 'col'))  122 us
    psum x1, waiting for transfers between devices, on_device(): lax.psum(right_acc.astype(jnp.bfloat16), 'row').astype(jnp.float32)  51.2 us
    reduce_scatter x1, waiting for transfers between devices, on_device(): lax.psum_scatter(projection_running_sum.astype(jnp.bfloat16), 'row', scat...  37.1 us
    psum x1, waiting for transfers between devices, from_root(): return lax.psum(block, axis)  32.9 us
    reduce_scatter x1, waiting for transfers between devices, on_device(): lax.psum_scatter(left_partial.astype(jnp.bfloat16), 'col', scatter_dimens...  21.9 us
    all_gather x1, waiting for transfers between devices, on_device(): right_every = lax.all_gather(right_rows, 'row', axis=1, tiled=True)  21.7 us
    reduce_scatter x1, waiting for transfers between devices, on_device(): lax.psum_scatter(proj_partial, 'col', scatter_dimension=0, tiled=True)  19.1 us
    all_gather x1, blocking collectives, on_device(): lax.all_gather(right_local, 'col', axis=0, tiled=True)  18 us
  transfers between devices with their start and end apart: 7, of which 7 were waited for; matrix products, arithmetic and copies ran while one was open for 3% of the time, Pallas kernels for 0%

commit v1 on v0

--- a/solution.py
+++ b/solution.py
@@ -1,7 +1,18 @@
+import functools
 import jax
 import jax.numpy as jnp
 from jax import lax
 from jax.sharding import PartitionSpec as P
+from jax.lax import psum
+
+
+def trace_meshes(my_tile, net_axis, comm_axis):
+    current_value = psum(my_tile, comm_axis)
+    far_arr = psum(current_value, net_axis)
+    return far_arr
+
+
+assign_quotas_by_axis = functools.partial(trace_meshes, net_axis="row", comm_axis="col")
 
 
 def from_root(block, axis, holder):
@@ -152,7 +163,7 @@
     )
     gain_part = jnp.sum(normed_derivative * normed_alignment, axis=(0, 1))
     bias_part = jnp.sum(pair_update_cotangent, axis=(0, 1), dtype=jnp.float32)
-    param_totals = lax.psum((weight_left, weight_right, gain_part, bias_part), ("row", "col"))
+    param_totals = assign_quotas_by_axis((weight_left, weight_right, gain_part, bias_part))
     proj_partial = lax.psum_scatter(
         projection_running_sum.astype(jnp.bfloat16), "row", scatter_dimension=0, tiled=True
     ).astype(jnp.float32)

time: 417 us -> 380 us (0.911)
  waiting for transfers between devices: 306 us -> 269 us
    psum x1 -> x2, waiting for transfers between devices: 122 us -> 86.5 us  [the longest x1 52.4 us: trace_meshes(): far_arr = psum(current_value, net_axis)]
  transfers between devices with their start and end apart: 7 -> 8, of which waited for: 7 -> 8; matrix products, arithmetic and copies ran while one was open for 3% -> 4% of each run, Pallas kernels for 0% -> 0%
where the time goes in v1:
time: 380 us; the launch traced here: 379 us
  waiting for transfers between devices  269 us (71%)
  blocking collectives  34.3 us (9%)
  local copies, waits for them, and re-layouts  20.9 us (6%)
  matrix products  18.1 us (5%)
  other arithmetic  18 us (5%)
  between operations  14.4 us (4%)
  loops' own time  4.07 us (1%)
    psum x1, waiting for transfers between devices, trace_meshes(): far_arr = psum(current_value, net_axis)  52.4 us
    psum x1, waiting for transfers between devices, on_device(): lax.psum(right_acc.astype(jnp.bfloat16), 'row').astype(jnp.float32)  51.2 us
    reduce_scatter x1, waiting for transfers between devices, on_device(): lax.psum_scatter(projection_running_sum.astype(jnp.bfloat16), 'row', scat...  35.5 us
    psum x1, waiting for transfers between devices, trace_meshes(): current_value = psum(my_tile, comm_axis)  34.2 us
    psum x1, waiting for transfers between devices, from_root(): return lax.psum(block, axis)  32.9 us
    reduce_scatter x1, waiting for transfers between devices, on_device(): lax.psum_scatter(left_partial.astype(jnp.bfloat16), 'col', scatter_dimens...  21.9 us
    all_gather x1, waiting for transfers between devices, on_device(): right_every = lax.all_gather(right_rows, 'row', axis=1, tiled=True)  21.7 us
    reduce_scatter x1, waiting for transfers between devices, on_device(): lax.psum_scatter(proj_partial, 'col', scatter_dimension=0, tiled=True)  19 us
  transfers between devices with their start and end apart: 8, of which 8 were waited for; matrix products, arithmetic and copies ran while one was open for 4% of the time, Pallas kernels for 0%

profile of v1, /device:TPU:0, one launch (start us, length us, event | category | flops | bytes accessed | tf_op | source)
XLA Modules:
  0.0 378.9 jit_solution(5912408314406808219)
XLA Ops:
  11.1 18.0 %all_gather.10 = bf16[128,16,32]{2,1,0:T(8,128)(2,1)} all-gather(bf16[32,16,32]{2,1,0:T(8,128)(2,1)S(1)} %bitcast.126), channel_id=1, replica_groups=mesh['row'=8,'col'=4] {'col'}, dimensions={0}, use_global_device_ids=true | all-gather | bytes 163840 | tf_op jit(solution)/shard_map/all_gather | solution.py:64
  29.6 16.3 %all_gather.9 = bf16[128,16,32]{2,1,0:T(8,128)(2,1)S(1)} all-gather(bf16[32,16,32]{2,1,0:T(8,128)(2,1)S(1)} %bitcast.127), channel_id=1, replica_groups=mesh['row'=8,'col'=4] {'col'}, dimensions={0}, use_global_device_ids=true | all-gather | bytes 163840 | tf_op jit(solution)/shard_map/all_gather | solution.py:63
  46.8 21.7 %all-gather.2.cloned.1.call-done = bf16[128,128,32]{2,1,0:T(8,128)(2,1)} async-done(((bf16[128,16,32]{2,1,0:T(8,128)(2,1)}), bf16[128,128,32]{2,1,0:T(8,128)(2,1)}) %all-gather.2.cloned.1.call-update) | async-done | bytes 1048592 | tf_op jit(solution)/shard_map/all_gather | solution.py:67
  68.5 1.3 constant_dynamic-slice_fusion.1
  69.8 1.8 copy.44
  71.6 32.6 %while.17 = (s32[]{:T(128)}, f32[128,32,32]{0,2,1:T(8,128)}, f32[1024,128]{1,0:T(8,128)S(1)}, bf16[2,8,32,128]{3,2,1,0:T(8,128)(2,1)}, bf16[2,128,8,32]{1,3,2,0:...) while((s32[]{:T(128)}, f32[128,32,32]{0,2,1:T(8,128)}, ...), condition=%wide.region_3.4_spmd.clone, body=%wide.region_2.3_spmd.clone.sunk | while | flops 404193280 | bytes 15928666 | solution.py:117
  71.6 1.2 dynamic_slice.46
  74.8 1.7 fusion.79
  76.5 2.2 reshape.95
  81.1 1.6 reshape.94
  82.7 1.5 fusion.78
  85.2 2.1 fusion.81
  87.4 1.2 dynamic_slice.46
  90.6 1.7 fusion.79
  92.2 2.2 reshape.95
  96.9 1.6 reshape.94
  98.5 2.6 fusion.78
  102.1 2.1 fusion.81
  104.2 1.8 convert_element_type.67
  106.1 2.1 copy.45
  108.9 51.2 %all-reduce.7.cloned.1.call-done = bf16[128,32,32]{0,2,1:T(8,128)(2,1)} async-done(((bf16[128,32,32]{0,2,1:T(8,128)(2,1)}), bf16[128,32,32]{0,2,1:T(8,128)(2,1)}) %all-reduce.7.cloned.1.call-update) | async-done | bytes 262160 | tf_op jit(solution)/shard_map/psum | solution.py:125
  160.1 1.6 fusion.28
  161.8 21.9 %reduce-scatter.4.cloned.1.call-done = bf16[32,16,32]{2,1,0:T(8,128)(2,1)} async-done(((bf16[128,16,32]{2,1,0:T(8,128)(2,1)}), bf16[32,16,32]{2,1,0:T(8,128)(2,1)}) %reduce-scatter.4.cloned.1.call-update) | async-done | bytes 32784 | tf_op jit(solution)/shard_map/reduce_scatter | solution.py:122
  184.8 1.7 convolution_bitcast_fusion.3
  186.5 32.9 %all-reduce.9.cloned.1.call-done = bf16[128,16,32]{0,2,1:T(8,128)(2,1)} async-done(((bf16[128,16,32]{0,2,1:T(8,128)(2,1)}), bf16[128,16,32]{0,2,1:T(8,128)(2,1)}) %all-reduce.9.cloned.1.call-update) | async-done | bytes 131088 | tf_op jit(solution)/shard_map/psum | solution.py:20
  222.5 34.2 %all-reduce.13.cloned.1.call-done = (f32[256,32]{0,1:T(8,128)}, f32[256,32]{0,1:T(8,128)}, f32[256]{0:T(256)}, f32[128]{0:T(128)}) async-done(((f32[256,32]{0,1:T(8,128)}, f32[256,32]{0,1:T(8,128)}, f32[256]{0:T(256)}, f32[128]{0:T(128)}), (f32[256,32]{0,1:T(8,128)}, f32[256,32]{0,1:T(8,128)}, f32[256]{0:T(256)}, f32[128]{0:T(128)})) %all-reduce.13.cloned.1.call-update) | async-done | bytes 67088 | tf_op jit(solution)/shard_map/psum | solution.py:10
  258.8 52.4 %all-reduce.11.cloned.1.call-done = (f32[256,32]{0,1:T(8,128)}, f32[256,32]{0,1:T(8,128)}, f32[256]{0:T(256)}, f32[128]{0:T(128)}) async-done(((f32[256,32]{0,1:T(8,128)}, f32[256,32]{0,1:T(8,128)}, f32[256]{0:T(256)}, f32[128]{0:T(128)}), (f32[256,32]{0,1:T(8,128)}, f32[256,32]{0,1:T(8,128)}, f32[256]{0:T(256)}, f32[128]{0:T(128)})) %all-reduce.11.cloned.1.call-update) | async-done | bytes 67088 | tf_op jit(solution)/shard_map/psum | solution.py:11
  312.3 1.4 broadcast_multiply_fusion
  313.8 35.5 %reduce-scatter.6.cloned.1.call-done = bf16[128,128]{1,0:T(8,128)(2,1)} async-done(((bf16[1024,128]{1,0:T(8,128)(2,1)}), bf16[128,128]{1,0:T(8,128)(2,1)}) %reduce-scatter.6.cloned.1.call-update) | async-done | bytes 32784 | tf_op jit(solution)/shard_map/reduce_scatter | solution.py:167
  349.2 1.4 convert_element_type.74
  351.7 19.0 %reduce-scatter.8.cloned.1.call-done = f32[32,128]{1,0:T(8,128)} async-done(((f32[128,128]{1,0:T(8,128)}), f32[32,128]{1,0:T(8,128)}) %reduce-scatter.8.cloned.1.call-update) | async-done | bytes 16400 | tf_op jit(solution)/shard_map/reduce_scatter | solution.py:170
  370.8 1.3 broadcast_multiply_fusion.2
  (101 shorter events, 21.2 us)
Async XLA Ops:
  7.2 3.6 copy-start
  7.2 22.1 %copy-start.12 = (bf16[256,32]{0,1:T(8,128)(2,1)S(1)}, bf16[256,32]{0,1:T(8,128)(2,1)}, u32[]{:S(2)}) copy-start(bf16[256,32]{0,1:T(8,128)(2,1)} %param.11) | copy-start | bytes 49156
  7.2 61.3 %all-gather.2.cloned.1.call-start = ((), (), s32[]{:S(2)}) async-start(), calls=%async_computation.3 | async-start | bytes 4718592 | tf_op jit(solution)/shard_map/all_gather | solution.py:67
  8.3 2.4 copy-start.8
  9.6 1.2 copy-start.10
  10.8 18.8 %copy-start.5 = (bf16[32,16,256]{2,1,0:T(8,128)(2,1)}, bf16[32,16,256]{2,1,0:T(8,128)(2,1)S(1)}, u32[]{:S(2)}) copy-start(bf16[32,16,256]{2,1,0:T(8,128)(2,1)S(1)} %fusion.21) | copy-start | bytes 786436
  29.1 131.0 %all-reduce.7.cloned.1.call-start = ((), (), s32[]{:S(2)}) async-start(), calls=%async_computation.5 | async-start | bytes 524288 | tf_op jit(solution)/shard_map/psum | solution.py:125
  45.9 25.7 %copy-start.1 = (bf16[1024,128]{1,0:T(8,128)(2,1)S(1)}, bf16[1024,128]{1,0:T(8,128)(2,1)}, u32[]{:S(2)}) copy-start(bf16[1024,128]{1,0:T(8,128)(2,1)} %param.13) | copy-start | bytes 786436
  80.0 0.8 copy-start.2
  82.7 1.6 copy-start.15
  82.7 1.8 copy-start.16
  84.3 3.1 copy-start.3
  84.6 0.7 copy-start.17
  95.8 0.8 copy-start.2
  98.5 2.6 copy-start.15
  98.5 2.9 copy-start.16
  101.1 3.1 copy-start.3
  101.4 0.7 copy-start.17
  104.2 4.1 %copy-start.7 = (bf16[16,32,128]{2,1,0:T(8,128)(2,1)S(1)}, bf16[16,32,128]{2,1,0:T(8,128)(2,1)}, u32[]{:S(2)}) copy-start(bf16[16,32,128]{2,1,0:T(8,128)(2,1)} %get-tuple-element.311) | copy-start | bytes 393220
  104.2 79.5 %copy-start.13 = (bf16[256,32]{0,1:T(8,128)(2,1)S(1)}, bf16[256,32]{0,1:T(8,128)(2,1)}, u32[]{:S(2)}) copy-start(bf16[256,32]{0,1:T(8,128)(2,1)} %param.11) | copy-start | bytes 49156
  104.2 80.6 %copy-start.6 = (bf16[32,16,256]{2,1,0:T(8,128)(2,1)S(1)}, bf16[32,16,256]{2,1,0:T(8,128)(2,1)}, u32[]{:S(2)}) copy-start(bf16[32,16,256]{2,1,0:T(8,128)(2,1)} %copy-done.5) | copy-start | bytes 786436
  106.1 115.3 %copy-start.14 = (f32[256]{0:T(256)S(1)}, f32[256]{0:T(256)}, u32[]{:S(2)}) copy-start(f32[256]{0:T(256)} %param.10) | copy-start | bytes 3076
  106.1 77.6 %reduce-scatter.4.cloned.1.call-start = ((), (), s32[]{:S(2)}) async-start(), calls=%async_computation.4 | async-start | bytes 655360 | tf_op jit(solution)/shard_map/reduce_scatter | solution.py:122
  108.2 113.4 %copy-start.4 = (bf16[32,16,256]{2,1,0:T(8,128)(2,1)S(1)}, bf16[32,16,256]{2,1,0:T(8,128)(2,1)}, u32[]{:S(2)}) copy-start(bf16[32,16,256]{2,1,0:T(8,128)(2,1)} %param.9) | copy-start | bytes 786436
  108.2 113.5 %copy-start.9 = (f32[32,16]{1,0:T(8,128)S(1)}, f32[32,16]{1,0:T(8,128)}, u32[]{:S(2)}) copy-start(f32[32,16]{1,0:T(8,128)} %copy-done.8) | copy-start | bytes 6148
  108.2 113.5 %copy-start.11 = (f32[32,16]{1,0:T(8,128)S(1)}, f32[32,16]{1,0:T(8,128)}, u32[]{:S(2)}) copy-start(f32[32,16]{1,0:T(8,128)} %copy-done.10) | copy-start | bytes 6148
  108.2 111.1 %all-reduce.9.cloned.1.call-start = ((), (), s32[]{:S(2)}) async-start(), calls=%async_computation.6 | async-start | bytes 262144 | tf_op jit(solution)/shard_map/psum | solution.py:20
  161.7 95.0 %all-reduce.13.cloned.1.call-start = ((), (), s32[]{:S(2)}) async-start(), calls=%async_computation.10 | async-start | bytes 134144 | tf_op jit(solution)/shard_map/psum | solution.py:10
  222.5 88.6 %all-reduce.11.cloned.1.call-start = ((), (), s32[]{:S(2)}) async-start(), calls=%async_computation.9 | async-start | bytes 134144 | tf_op jit(solution)/shard_map/psum | solution.py:11
  256.8 92.4 %reduce-scatter.6.cloned.1.call-start = ((), (), s32[]{:S(2)}) async-start(), calls=%async_computation.7 | async-start | bytes 294912 | tf_op jit(solution)/shard_map/reduce_scatter | solution.py:167
  257.6 113.2 %reduce-scatter.8.cloned.1.call-start = ((), (), s32[]{:S(2)}) async-start(), calls=%async_computation.8 | async-start | bytes 81920 | tf_op jit(solution)/shard_map/reduce_scatter | solution.py:170
Sparse Core Ops, SparseCore 0:
  29.3 39.2 all-gather.1
  106.2 53.8 all-reduce.6
  162.4 21.2 reduce-scatter.3
  186.4 32.8 all-reduce.8
  222.6 34.0 all-reduce.12
  260.1 50.9 all-reduce.10
  314.1 35.0 reduce-scatter.5
  351.5 19.2 reduce-scatter.7
